TPU v7x, 32 devices: a whole 2x2x4 slice. The times are simulated.
32 devices in a mesh: dp: 4 (over z), sp: 8 (over y, x, core).
Axes of the slice: x: 2, y: 2, z: 4, core: 2. Of those that a mesh axis runs over, the one named last changes fastest.
Arguments:
- queries_in: bfloat16 [8, 8192, 16, 128], P('dp', 'sp'), may hold values from -6 to 6
- keys_in: bfloat16 [8, 8192, 16, 128], P('dp', 'sp'), may hold values from -6 to 6
- values_in: bfloat16 [8, 8192, 16, 128], P('dp', 'sp'), may hold values from -6 to 6
- out_weight: bfloat16 [2048, 2048], P('dp'), may hold values from -0.125 to 0.125
Outputs:
- block_out: bfloat16 [8, 8192, 2048], P('dp', 'sp')
All inputs are finite; a program needn't handle non-finite values.
Results may differ from a plain program's by a relative error of at most 0.006.
Values may be sent and summed in bfloat16 or wider, within the bound.
A program may use at most 320 MiB of HBM per device.

v0:
```python
import functools

import jax
import jax.numpy as jnp
from jax import lax
from jax.experimental import pallas as pl
from jax.experimental.pallas import tpu as pltpu
from jax.sharding import PartitionSpec as P

MESH = pl.DeviceIdType.MESH
SLOTS = 3
CHUNK = 256
TILE = 512


def feature_map(values):
    wide = values.astype(jnp.float32)
    return (wide * wide + 0.1).astype(jnp.bfloat16)


def gather_kernel(
    groups, count, chunk, batch, tokens, heads, size,
    k_ref, v_ref, w_ref, state_ref, mass_ref, wide_ref,
    k_buf, v_buf, total, sums, core_in, half_out, half_in, sums_out, sums_in,
    load_sem, own_sem, z_send, z_recv, w_send, w_recv, s_send, s_recv,
):
    depth, lanes = groups
    places = lanes // 2
    levels = places.bit_length() - 1
    d, s = lax.axis_index("dp"), lax.axis_index("sp")
    core, place = s % 2, s // 2
    piece = core * places + place
    rows = w_ref.shape[0]
    part = rows // lanes
    half_width = w_ref.shape[1] // 2
    steps = batch * tokens // chunk
    per_batch = tokens // chunk

    def flip(value, bit):
        return value + (1 << bit) - 2 * (1 << bit) * ((value // (1 << bit)) % 2)

    partners = [flip(s, bit) for bit in range(levels + 1)]

    def to_lane(bit):
        return {"sp": partners[bit]}

    barrier = pltpu.get_barrier_semaphore()
    for bit in range(levels + 1):
        pl.semaphore_signal(barrier, inc=1, device_id=to_lane(bit), device_id_type=MESH)
    for k in (1, depth - 1):
        pl.semaphore_signal(
            barrier, inc=1, device_id={"dp": (d + k) % depth}, device_id_type=MESH
        )

    def load(i):
        half = steps // 2
        side = jnp.where(i < half, 1 - core, core)
        at = side * half + i % half
        b, t = at // per_batch, at % per_batch
        slot = i % SLOTS
        return (
            pltpu.make_async_copy(
                k_ref.at[b, pl.ds(t * chunk, chunk)], k_buf.at[slot], load_sem.at[0, slot]
            ),
            pltpu.make_async_copy(
                v_ref.at[b, pl.ds(t * chunk, chunk)], v_buf.at[slot], load_sem.at[1, slot]
            ),
        )

    for i in range(min(SLOTS - 1, steps)):
        for copy in load(i):
            copy.start()
    total[...] = jnp.zeros_like(total)
    sums[...] = jnp.zeros_like(sums)
    pl.semaphore_wait(barrier, levels + 3)

    def origin(way, hop):
        return d - hop if way == 0 else d + hop

    def inside(place_on_dp):
        return jnp.logical_and(place_on_dp >= 0, place_on_dp < depth)

    def z_copy(way, hop):
        at = pl.ds(origin(way, hop - 1) * rows + piece * part, part)
        return pltpu.make_async_remote_copy(
            src_ref=w_ref.at[pl.ds(piece * part, part)] if hop == 1 else wide_ref.at[at],
            dst_ref=wide_ref.at[at],
            send_sem=z_send.at[way, hop],
            recv_sem=z_recv.at[way, hop],
            device_id={"dp": (d + (1 if way == 0 else depth - 1)) % depth},
            device_id_type=MESH,
        )

    def sends(way, hop):
        return jnp.logical_and(inside(origin(way, hop - 1)), inside(origin(way, -1)))

    def z_start(hop):
        for way in range(2):
            pl.when(sends(way, hop))(lambda way=way: z_copy(way, hop).start())

    z_start(1)
    own = pltpu.make_async_copy(w_ref, wide_ref.at[pl.ds(d * rows, rows)], own_sem)
    own.start()

    def orders(side):
        return list(range(levels)) if side == 0 else list(range(levels))[::-1]

    def w_copies(way, hop, stage):
        first = origin(way, hop) * rows
        k = way * depth + hop
        if stage == levels:
            block = wide_ref.at[pl.ds(first + core * places * part, places * part)]
            slot = 2 * (places - 1)
            return [
                pltpu.make_async_remote_copy(
                    src_ref=block, dst_ref=block, send_sem=w_send.at[k, slot],
                    recv_sem=w_recv.at[k, slot], device_id=to_lane(0), device_id_type=MESH,
                )
            ]
        copies = []
        for side in range(2):
            bits = orders(side)
            for subset in range(1 << stage):
                member = place
                for j in range(stage):
                    if subset >> j & 1:
                        member = flip(member, bits[j])
                slot = side * (places - 1) + (1 << stage) - 1 + subset
                block = wide_ref.at[
                    pl.ds(first + (core * places + member) * part, part),
                    pl.ds(side * half_width, half_width),
                ]
                copies.append(
                    pltpu.make_async_remote_copy(
                        src_ref=block, dst_ref=block, send_sem=w_send.at[k, slot],
                        recv_sem=w_recv.at[k, slot], device_id=to_lane(bits[stage] + 1),
                        device_id_type=MESH,
                    )
                )
        return copies

    def w_step(hop, stage):
        def arrived(way):
            if stage == 0:
                at = pl.ds(origin(way, hop) * rows + piece * part, part)
                pltpu.make_async_remote_copy(
                    src_ref=wide_ref.at[at], dst_ref=wide_ref.at[at],
                    send_sem=z_send.at[way, hop], recv_sem=z_recv.at[way, hop],
                    device_id={"dp": (d + 1) % depth}, device_id_type=MESH,
                ).wait_recv()
            else:
                for copy in w_copies(way, hop, stage - 1):
                    copy.wait_recv()

        def forward(way):
            for copy in w_copies(way, hop, stage):
                copy.start()

        for act in (arrived, None, forward):
            if act is None:
                if stage == 0 and hop + 1 < depth:
                    z_start(hop + 1)
                continue
            for way in range(2):
                pl.when(inside(origin(way, hop)))(functools.partial(act, way))

    todo = [(hop, stage) for hop in range(1, depth) for stage in range(levels + 1)]
    todo.sort(key=lambda item: (item[0] + item[1], item[0]))
    early = {steps // 2: todo.pop(0), steps - 2: todo.pop(0), steps - 1: todo.pop(0)}

    held = total.shape[0] // 2
    core_copy = pltpu.make_async_remote_copy(
        src_ref=total.at[pl.ds((1 - core) * held, held)], dst_ref=core_in,
        send_sem=s_send.at[0], recv_sem=s_recv.at[0],
        device_id=to_lane(0), device_id_type=MESH,
    )

    def step(i, carry):
        @pl.when(i + SLOTS - 1 < steps)
        def _():
            for copy in load(i + SLOTS - 1):
                copy.start()

        @pl.when(i == steps // 2)
        def _():
            core_copy.start()

        for moment, item in early.items():
            pl.when(i == moment)(functools.partial(w_step, *item))

        for copy in load(i):
            copy.wait()
        slot = i % SLOTS
        half = steps // 2
        b = (jnp.where(i < half, 1 - core, core) * half + i % half) // per_batch
        k_feature = feature_map(k_buf[slot])
        sums[pl.ds(b * heads, heads), :] += jnp.sum(k_feature.astype(jnp.float32), axis=0)
        k_heads = pltpu.einshape("thd->htd", k_feature)
        v_heads = pltpu.einshape("thd->htd", v_buf[slot])
        for h in range(heads):
            at = pl.ds((b * heads + h) * size, size)
            total[at, :] += lax.dot_general(
                k_heads[h], v_heads[h], (((0,), (0,)), ((), ())),
                preferred_element_type=jnp.float32,
            )
        return carry

    lax.fori_loop(0, steps, step, 0)

    def mass_copy(stage):
        bit = 0 if stage == 0 else orders(0)[stage - 1] + 1
        return pltpu.make_async_remote_copy(
            src_ref=sums_out.at[stage], dst_ref=sums_in.at[stage],
            send_sem=s_send.at[1 + stage], recv_sem=s_recv.at[1 + stage],
            device_id=to_lane(bit), device_id_type=MESH,
        )

    def mass_send(stage):
        sums_out[stage] = sums[...]
        mass_copy(stage).start()

    def mass_take(stage):
        mass_copy(stage).wait()
        sums[...] += sums_in[stage]

    mass_send(0)
    core_copy.wait()
    mine = pl.ds(core * held, held)
    total[mine, :] += core_in[...]
    mass_take(0)

    quarter = held // 2
    starts = [[core * held + side * quarter] for side in range(2)]

    def reduce_copy(stage, side):
        length = quarter >> (stage + 1)
        slot = 2 + levels + 2 * stage + side
        base = side * quarter + quarter - 2 * length
        return pltpu.make_async_remote_copy(
            src_ref=half_out.at[pl.ds(base, length)], dst_ref=half_in.at[pl.ds(base, length)],
            send_sem=s_send.at[slot], recv_sem=s_recv.at[slot],
            device_id=to_lane(orders(side)[stage] + 1), device_id_type=MESH,
        )

    def reduce_send(stage):
        length = quarter >> (stage + 1)
        for side in range(2):
            first = starts[side][stage]
            upper = (place // (1 << orders(side)[stage])) % 2
            keep, give = first + upper * length, first + (1 - upper) * length
            starts[side].append(keep)
            base = side * quarter + quarter - 2 * length
            half_out[pl.ds(base, length), :] = total[pl.ds(give, length), :].astype(jnp.bfloat16)
            reduce_copy(stage, side).start()
        mass_send(stage + 1)

    def reduce_take(stage):
        length = quarter >> (stage + 1)
        for side in range(2):
            base = side * quarter + quarter - 2 * length
            reduce_copy(stage, side).wait()
            total[pl.ds(starts[side][stage + 1], length), :] += half_in[
                pl.ds(base, length), :
            ].astype(jnp.float32)
        mass_take(stage + 1)

    def spread_copy(stage, side):
        length = quarter >> (stage + 1)
        block = state_ref.at[pl.ds(starts[side][stage + 1], length)]
        slot = 2 + 3 * levels + 2 * stage + side
        return pltpu.make_async_remote_copy(
            src_ref=block, dst_ref=block, send_sem=s_send.at[slot], recv_sem=s_recv.at[slot],
            device_id=to_lane(orders(side)[stage] + 1), device_id_type=MESH,
        )

    final_copy = pltpu.make_async_remote_copy(
        src_ref=state_ref.at[mine], dst_ref=state_ref.at[mine],
        send_sem=s_send.at[2 + 5 * levels], recv_sem=s_recv.at[2 + 5 * levels],
        device_id=to_lane(0), device_id_type=MESH,
    )

    def next_w(amount=1):
        for _ in range(amount):
            if todo:
                w_step(*todo.pop(0))

    for stage in range(levels):
        reduce_send(stage)
        next_w(2 - stage)
        reduce_take(stage)
    length = quarter >> levels
    for side in range(2):
        at = pl.ds(starts[side][levels], length)
        state_ref[at, :] = (total[at, :] / count).astype(jnp.bfloat16)
    mass_ref[...] = sums[...] / count
    for stage in reversed(range(levels)):
        for side in range(2):
            spread_copy(stage, side).start()
        next_w()
        for side in range(2):
            spread_copy(stage, side).wait()
    final_copy.start()
    next_w(len(todo))
    final_copy.wait()
    for hop in range(1, depth):
        for way in range(2):
            pl.when(sends(way, hop))(lambda way=way, hop=hop: z_copy(way, hop).wait_send())

            @pl.when(inside(origin(way, hop)))
            def _(way=way, hop=hop):
                for stage in range(levels + 1):
                    for copy in w_copies(way, hop, stage):
                        copy.wait_send()
                        if stage == levels:
                            copy.wait_recv()

    own.wait()


def gather(queries, keys_in, values_in, out_weight, count):
    batch, tokens, heads, size = keys_in.shape
    depth, lanes = lax.axis_size("dp"), lax.axis_size("sp")
    places = lanes // 2
    levels = places.bit_length() - 1
    rows, width = out_weight.shape
    area = batch * heads * size
    chunk = min(CHUNK, tokens)
    any_space = pl.BlockSpec(memory_space=pl.ANY)
    vmem = pl.BlockSpec(memory_space=pltpu.VMEM)
    dma = pltpu.SemaphoreType.DMA
    f32, bf16 = jnp.float32, jnp.bfloat16
    return pl.pallas_call(
        functools.partial(
            gather_kernel, (depth, lanes), count, chunk, batch, tokens, heads, size
        ),
        out_shape=(
            jax.ShapeDtypeStruct((area, size), bf16),
            jax.ShapeDtypeStruct((batch * heads, size), f32),
            jax.ShapeDtypeStruct((depth * rows, width), bf16),
        ),
        in_specs=[any_space, any_space, vmem],
        out_specs=(vmem, vmem, any_space),
        scratch_shapes=[
            pltpu.VMEM((SLOTS, chunk, heads, size), bf16),
            pltpu.VMEM((SLOTS, chunk, heads, size), bf16),
            pltpu.VMEM((area, size), f32),
            pltpu.VMEM((batch * heads, size), f32),
            pltpu.VMEM((area // 2, size), f32),
            pltpu.VMEM((area // 2, size), bf16),
            pltpu.VMEM((area // 2, size), bf16),
            pltpu.VMEM((levels + 1, batch * heads, size), f32),
            pltpu.VMEM((levels + 1, batch * heads, size), f32),
            dma((2, SLOTS)),
            dma,
            dma((2, depth)),
            dma((2, depth)),
            dma((2 * depth, 2 * places - 1)),
            dma((2 * depth, 2 * places - 1)),
            dma((3 + 5 * levels,)),
            dma((3 + 5 * levels,)),
        ],
        compiler_params=pltpu.CompilerParams(
            collective_id=0, has_side_effects=True, vmem_limit_bytes=60 * 2**20
        ),
    )(keys_in, values_in, out_weight)


def project_kernel(
    count, per_batch, q_ref, state_ref, mass_ref, w_hbm, out_ref, table, mixed, w_ref, w_sem
):
    heads, size = q_ref.shape[1:]
    f32, bf16 = jnp.float32, jnp.bfloat16
    i, last = pl.program_id(0), pl.num_programs(0) - 1
    load = pltpu.make_async_copy(w_hbm, w_ref, w_sem)

    pl.when(i == 0)(load.start)

    @pl.when(jnp.logical_and(i % per_batch == 0, i < last))
    def _():
        b = i // per_batch
        for h in range(heads):
            line = mass_ref[pl.ds(b * heads + h, 1), :]
            column = jnp.transpose(jnp.broadcast_to(line, (size, size)))
            high = column.astype(bf16)
            table[h, :size, :size] = state_ref[pl.ds((b * heads + h) * size, size), :]
            table[h, :size, size:] = high
            table[h, size:, :size] = jnp.zeros((size, size), bf16)
            table[h, size:, size:] = (column - high.astype(f32)).astype(bf16)

    def read(slot):
        q_heads = pltpu.einshape("thd->htd", feature_map(q_ref[...]))
        for h in range(heads):
            feature = q_heads[h]
            both = jnp.dot(
                jnp.concatenate([feature, feature], axis=1), table[h], preferred_element_type=f32
            )
            top = both[:, :size] / (both[:, size:] + 0.001)
            mixed[slot, :, h * size : (h + 1) * size] = (top * count**0.5).astype(bf16)

    def finish(slot):
        out_ref[...] = jnp.dot(mixed[slot], w_ref[...], preferred_element_type=f32).astype(bf16)

    @pl.when(i == 0)
    def _():
        read(0)
        load.wait()

    for slot in range(2):
        @pl.when(jnp.logical_and(i % 2 == slot, jnp.logical_and(i > 0, i < last)))
        def _():
            finish(1 - slot)
            read(slot)

        @pl.when(jnp.logical_and(i % 2 == slot, i == last))
        def _():
            finish(1 - slot)


def project(queries_in, state, mass, wide, count):
    batch, tokens, heads, size = queries_in.shape
    width = wide.shape[1]
    tile = min(TILE, tokens)
    tiles = batch * tokens // tile
    vmem = pl.BlockSpec(memory_space=pltpu.VMEM)
    out = pl.pallas_call(
        functools.partial(project_kernel, count, tokens // tile),
        grid=(tiles + 1,),
        out_shape=jax.ShapeDtypeStruct((batch * tokens, width), jnp.bfloat16),
        in_specs=[
            pl.BlockSpec((tile, heads, size), lambda i: (jnp.minimum(i, tiles - 1), 0, 0)),
            vmem,
            vmem,
            pl.BlockSpec(memory_space=pl.ANY),
        ],
        out_specs=pl.BlockSpec((tile, width), lambda i: (jnp.maximum(i - 1, 0), 0)),
        scratch_shapes=[
            pltpu.VMEM((heads, 2 * size, 2 * size), jnp.bfloat16),
            pltpu.VMEM((2, tile, heads * size), jnp.bfloat16),
            pltpu.VMEM(wide.shape, jnp.bfloat16),
            pltpu.SemaphoreType.DMA,
        ],
        compiler_params=pltpu.CompilerParams(
            dimension_semantics=("arbitrary",), vmem_limit_bytes=60 * 2**20
        ),
    )(queries_in.reshape(batch * tokens, heads, size), state, mass, wide)
    return out.reshape(batch, tokens, width)


def on_device(queries_in, keys_in, values_in, out_weight):
    count = queries_in.shape[1] * lax.axis_size("sp")
    state, mass, wide = gather(queries_in, keys_in, values_in, out_weight, count)
    return project(queries_in, state, mass, wide, count)


def solution(mesh):
    placed = (
        P("dp", "sp", None, None),
        P("dp", "sp", None, None),
        P("dp", "sp", None, None),
        P("dp", None),
    )
    return jax.shard_map(
        on_device, mesh=mesh, in_specs=placed, out_specs=P("dp", "sp", None), check_vma=False
    )
```

profile of v0, /device:TPU:9, one launch (start us, length us, event | category | flops | bytes accessed | tf_op | source)
XLA Modules:
  0.0 87.9 jit_solution(5737382494464967032)
XLA Ops:
  0.0 57.5 %shard_map.46 = (bf16[4096,128]{1,0:T(8,128)(2,1)}, f32[32,128]{1,0:T(8,128)}, bf16[2048,2048]{1,0:T(8,128)(2,1)}) custom-call(bf16[2,1024,16,128]{3,2,1,0:T(8,128)(2,1)} %k_ref.1, bf16[2,1024,16,128]{3,2,1,0:T(8,128)(2,1)} %v_ref.1, bf16[512,2048]{1,0:T(8,128)(2,1)} %w_ref.1), custom_call_target="tpu_custom_call" | custom-call | tf_op jit(solution)/shard_map/pallas_call | solution.py:332
  57.5 30.2 %shard_map.47 = bf16[2048,2048]{1,0:T(8,128)(2,1)} custom-call(bf16[2048,16,128]{2,1,0:T(8,128)(2,1)} %bitcast.2, bf16[4096,128]{1,0:T(8,128)(2,1)} %get-tuple-element.8.state_ref, f32[32,128]{1,0:T(8,128)} %get-tuple-element.9.mass_ref, bf16[2048,2048]{1,0:T(8,128)(2,1)} %get-tuple-element.10.w_hbm), custom_call_target="tpu_custom_call" | custom-call | tf_op jit(solution)/shard_map/pallas_call | solution.py:425
where the time goes:
time: 88.1 us; the launch traced here: 87.9 us
  Pallas kernels  87.8 us (100%)
    pallas_call x1, Pallas kernels, gather(): pl.pallas_call(functools.partial(gather_kernel, (depth, lanes), count, ch...  57.5 us
    pallas_call x1, Pallas kernels, project(): pl.pallas_call(functools.partial(project_kernel, count, tokens // tile),...  30.2 us

commit v1 on v0

v1 whole, which is shorter than its diff:
```python
import functools

import jax
import jax.numpy as jnp
from jax import lax
from jax.experimental import pallas as pl
from jax.experimental.pallas import tpu as pltpu
from jax.sharding import PartitionSpec as P

MESH = pl.DeviceIdType.MESH
SLOTS = 3
TILE = 256
PITCH = 24
EXTRA = 16


def feature_map(values):
    wide = values.astype(jnp.float32)
    return wide * wide + 0.1


def split_mass(mass):
    high = mass.astype(jnp.bfloat16).astype(jnp.float32)
    row = lax.broadcasted_iota(jnp.int32, mass.shape, mass.ndim - 2)
    return jnp.where(row % 2 == 0, high, mass - high).astype(jnp.bfloat16)


def gather_kernel(
    groups, count, tile, batch, tokens, heads, size,
    q_ref, k_ref, v_ref, w_ref, mixed_ref, wide_ref,
    k_buf, v_buf, q_buf, mixed_buf, rel_k, rel_v, total, core_in, out_buf, in_buf,
    final, table, w_all,
    load_sem, q_sem, mixed_sem, own_sem, wide_sem,
    z_send, z_recv, n_send, n_recv, p_send, p_recv, m_send, m_recv,
    c_send, c_recv, r_send, r_recv, g_send, g_recv, f_send, f_recv,
):
    f32, bf16 = jnp.float32, jnp.bfloat16
    depth, lanes = groups
    places = lanes // 2
    levels = places.bit_length() - 1
    d, s = lax.axis_index("dp"), lax.axis_index("sp")
    core, place = s % 2, s // 2
    rows, width = w_ref.shape
    part, half_width = rows // 4, width // 2
    per_batch = tokens // tile
    steps = batch * per_batch
    held = heads // 2
    piece = held // places
    root = count**0.5

    def flip(value, bit):
        return value + (1 << bit) - 2 * (1 << bit) * ((value // (1 << bit)) % 2)

    def peer_place(k):
        other = place
        for bit in range(levels):
            if k >> bit & 1:
                other = flip(other, bit)
        return other

    partner = {"sp": flip(s, 0)}
    peers = [{"sp": 2 * peer_place(k) + core} for k in range(1, places)]
    sides = [{"sp": flip(s, 1)}, {"sp": flip(s, levels)}]
    parity = place % 2
    if levels > 1:
        parity = (parity + (place // (1 << (levels - 1))) % 2) % 2
    quarter, across = parity * 2 + core, (1 - parity) * 2 + core

    barrier = pltpu.get_barrier_semaphore()
    for device in [partner] + peers + [{"dp": (d + k) % depth} for k in (1, depth - 1)]:
        pl.semaphore_signal(barrier, inc=1, device_id=device, device_id_type=MESH)

    def load(i):
        b, t, slot = i // per_batch, i % per_batch, i % SLOTS
        at = pl.ds(t * tile, tile)
        return (
            pltpu.make_async_copy(k_ref.at[b, at], k_buf.at[slot], load_sem.at[0, slot]),
            pltpu.make_async_copy(v_ref.at[b, at], v_buf.at[slot], load_sem.at[1, slot]),
        )

    def load_q(i):
        b, t, slot = i // per_batch, i % per_batch, i % SLOTS
        return pltpu.make_async_copy(
            q_ref.at[b, pl.ds(t * tile, tile)], q_buf.at[slot], q_sem.at[slot]
        )

    def store_mixed(i):
        return pltpu.make_async_copy(
            mixed_buf.at[i % 2], mixed_ref.at[pl.ds(i * tile, tile)], mixed_sem.at[i % 2]
        )

    for i in range(min(SLOTS - 1, steps)):
        for copy in load(i):
            copy.start()
    own = pltpu.make_async_copy(w_ref, w_all.at[d], own_sem)
    own.start()
    total[...] = jnp.zeros_like(total)
    table[...] = jnp.zeros_like(table)
    pl.semaphore_wait(barrier, places + 2)

    def origin(way, hop):
        return d - hop if way == 0 else d + hop

    def inside(place_on_dp):
        return jnp.logical_and(place_on_dp >= 0, place_on_dp < depth)

    def sends(way, hop):
        return jnp.logical_and(inside(origin(way, hop - 1)), inside(origin(way, -1)))

    def block(from_dp, index, side):
        return w_all.at[
            from_dp, pl.ds(index * part, part), pl.ds(side * half_width, half_width)
        ]

    def z_copy(way, hop, side):
        target = block(origin(way, hop - 1), quarter, side)
        source = target
        if hop == 1:
            source = w_ref.at[
                pl.ds(quarter * part, part), pl.ds(side * half_width, half_width)
            ]
        return pltpu.make_async_remote_copy(
            src_ref=source, dst_ref=target,
            send_sem=z_send.at[way, hop, side], recv_sem=z_recv.at[way, hop, side],
            device_id={"dp": (d + (1 if way == 0 else depth - 1)) % depth},
            device_id_type=MESH,
        )

    def z_arrival(way, hop, side):
        target = block(origin(way, hop), quarter, side)
        return pltpu.make_async_remote_copy(
            src_ref=target, dst_ref=target,
            send_sem=z_send.at[way, hop, side], recv_sem=z_recv.at[way, hop, side],
            device_id={"dp": (d + 1) % depth}, device_id_type=MESH,
        )

    def spread(way, hop, side, index, send, recv, device):
        target = block(origin(way, hop), index, side)
        return pltpu.make_async_remote_copy(
            src_ref=target, dst_ref=target,
            send_sem=send.at[way, hop, side], recv_sem=recv.at[way, hop, side],
            device_id=device, device_id_type=MESH,
        )

    def n_copy(way, hop, side):
        return spread(way, hop, side, quarter, n_send, n_recv, sides[side])

    def p_copy(way, hop, side):
        return spread(way, hop, side, quarter, p_send, p_recv, partner)

    def m_copy(way, hop, side):
        return spread(way, hop, side, across, m_send, m_recv, partner)

    def each_way(hop, act):
        for way in range(2):
            pl.when(inside(origin(way, hop)))(functools.partial(act, way))

    def z_event(hop, side):
        each_way(hop, lambda way: z_arrival(way, hop, side).wait_recv())
        if hop + 1 < depth:
            for way in range(2):
                pl.when(sends(way, hop + 1))(
                    lambda way=way: z_copy(way, hop + 1, side).start()
                )

        def forward(way):
            n_copy(way, hop, side).start()
            p_copy(way, hop, side).start()

        each_way(hop, forward)

    def n_event(hop, side):
        def act(way):
            n_copy(way, hop, side).wait_recv()
            m_copy(way, hop, side).start()

        each_way(hop, act)

    def wide_copy(way, hop):
        at = origin(way, hop)
        return pltpu.make_async_copy(
            w_all.at[at], wide_ref.at[pl.ds(at * rows, rows)], wide_sem.at[way, hop]
        )

    def f_event(hop):
        def act(way):
            for side in range(2):
                p_copy(way, hop, side).wait_recv()
                m_copy(way, hop, side).wait_recv()
            wide_copy(way, hop).start()

        each_way(hop, act)

    def w_end():
        for hop in range(1, depth):
            for way in range(2):
                for side in range(2):
                    pl.when(sends(way, hop))(
                        lambda way=way, hop=hop, side=side: z_copy(way, hop, side).wait_send()
                    )

            def act(way, hop=hop):
                for side in range(2):
                    for make in (n_copy, p_copy, m_copy):
                        make(way, hop, side).wait_send()
                wide_copy(way, hop).wait()

            each_way(hop, act)
        own_out.wait()

    for side in range(2):
        for way in range(2):
            pl.when(sends(way, 1))(lambda way=way, side=side: z_copy(way, 1, side).start())

    def c_copy(b):
        return pltpu.make_async_remote_copy(
            src_ref=total.at[b, pl.ds((1 - core) * held, held)], dst_ref=core_in.at[b],
            send_sem=c_send.at[b], recv_sem=c_recv.at[b],
            device_id=partner, device_id_type=MESH,
        )

    def r_copy(b, k):
        return pltpu.make_async_remote_copy(
            src_ref=out_buf.at[b, pl.ds(peer_place(k) * piece, piece)],
            dst_ref=in_buf.at[b, k - 1],
            send_sem=r_send.at[b, k], recv_sem=r_recv.at[b, k],
            device_id=peers[k - 1], device_id_type=MESH,
        )

    def g_copy(b, k):
        at = final.at[b, pl.ds(core * held + place * piece, piece)]
        return pltpu.make_async_remote_copy(
            src_ref=at, dst_ref=at, send_sem=g_send.at[b, k], recv_sem=g_recv.at[b, k],
            device_id=peers[k - 1], device_id_type=MESH,
        )

    def f_copy(b):
        at = final.at[b, pl.ds(core * held, held)]
        return pltpu.make_async_remote_copy(
            src_ref=at, dst_ref=at, send_sem=f_send.at[b], recv_sem=f_recv.at[b],
            device_id=partner, device_id_type=MESH,
        )

    def x_add(b):
        c_copy(b).wait()
        mine = pl.ds(core * held, held)
        summed = total[b, mine] + core_in[b]
        total[b, mine] = summed
        out_buf[b, :, :size] = summed[:, :size].astype(bf16)
        out_buf[b, :, size:] = split_mass(summed[:, size:])
        for k in range(1, places):
            r_copy(b, k).start()

    def x_sum(b):
        mine = pl.ds(core * held + place * piece, piece)
        state, mass = total[b, mine, :size], total[b, mine, size:]
        for k in range(1, places):
            r_copy(b, k).wait_recv()
            state += in_buf[b, k - 1, :, :size].astype(f32)
            pair = in_buf[b, k - 1, :, size:].astype(f32)
            mass += pair[:, :1] + pair[:, 1:2]
        final[b, mine, :size] = (state / count).astype(bf16)
        final[b, mine, size:] = split_mass(mass / count / root)
        for k in range(1, places):
            g_copy(b, k).start()

    def x_share(b):
        for k in range(1, places):
            g_copy(b, k).wait_recv()
        f_copy(b).start()

    def x_table(b):
        f_copy(b).wait_recv()
        for h in range(heads):
            pair = final[b, h, size:].astype(f32)
            table[h, :size, :size] = final[b, h, :size]
            table[h, size:, :size] = jnp.broadcast_to(pair[:1], (size, size)).astype(bf16)
            table[h, size:, size:] = jnp.broadcast_to(pair[1:2], (size, size)).astype(bf16)

    def x_end(b):
        for k in range(1, places):
            r_copy(b, k).wait_send()
            g_copy(b, k).wait_send()
        f_copy(b).wait_send()

    def relay(buffer, values):
        buffer.reshape(tile, PITCH, size)[:, :heads, :] = values

    def pick(buffer, h):
        return buffer[pl.ds(h, tile, stride=PITCH), :].astype(bf16)

    ones = jnp.ones((EXTRA, tile), bf16)

    def fold(i):
        slot, b = i % SLOTS, i // per_batch
        relay(rel_k, feature_map(k_buf[slot]))
        relay(rel_v, v_buf[slot].astype(f32))
        for h in range(heads):
            left = jnp.concatenate([jnp.transpose(pick(rel_v, h)), ones], axis=0)
            total[b, h] += jnp.dot(left, pick(rel_k, h), preferred_element_type=f32)

    def read(i):
        relay(rel_k, feature_map(q_buf[i % SLOTS]))
        for h in range(heads):
            feature = pick(rel_k, h)
            both = lax.dot_general(
                jnp.concatenate([feature, feature], axis=1), table[h],
                (((1,), (1,)), ((), ())), preferred_element_type=f32,
            )
            top = both[:, :size] / (both[:, size:] + 0.001 / root)
            mixed_buf[i % 2, :, h * size : (h + 1) * size] = top.astype(bf16)

    def at_step(i, events):
        for moment, items in events.items():
            def run(items=items):
                for item in items:
                    item()

            pl.when(i == moment)(run)

    def make(function, *args):
        return functools.partial(function, *args)

    first = per_batch
    fold_events = {
        first: [lambda: c_copy(0).start(), make(z_event, 1, 0)],
        first + 1: [make(x_add, 0)],
        first + 2: [make(z_event, 1, 1)],
        first + 3: [make(x_sum, 0), make(n_event, 1, 0)],
    }

    def fold_step(i, carry):
        @pl.when(i + SLOTS - 1 < steps)
        def _():
            for copy in load(i + SLOTS - 1):
                copy.start()

        @pl.when(i + SLOTS - 1 >= steps)
        def _():
            load_q(i + SLOTS - 1 - steps).start()

        at_step(i, fold_events)
        for copy in load(i):
            copy.wait()
        fold(i)
        return carry

    lax.fori_loop(0, steps, fold_step, 0)
    own.wait()
    own_out = pltpu.make_async_copy(w_all.at[d], wide_ref.at[pl.ds(d * rows, rows)], own_sem)
    own_out.start()
    c_copy(1).start()
    x_share(0)
    n_event(1, 1)
    z_event(2, 0)
    x_add(1)
    x_table(0)

    last = per_batch
    read_events = {
        1: [make(z_event, 2, 1), make(x_sum, 1), make(n_event, 2, 0)],
        2: [make(f_event, 1), make(z_event, 3, 0)],
        3: [make(x_share, 1), make(n_event, 2, 1)],
        last: [make(x_table, 1), make(z_event, 3, 1)],
        last + 1: [make(n_event, 3, 0), make(f_event, 2)],
        last + 3: [make(n_event, 3, 1)],
    }

    def read_step(i, carry):
        @pl.when(i + SLOTS - 1 < steps)
        def _():
            load_q(i + SLOTS - 1).start()

        at_step(i, read_events)
        load_q(i).wait()
        pl.when(i > 1)(lambda: store_mixed(i - 2).wait())
        read(i)
        store_mixed(i).start()
        return carry

    lax.fori_loop(0, steps, read_step, 0)
    for hop in range(4, depth):
        for side in range(2):
            z_event(hop, side)
        for side in range(2):
            n_event(hop, side)
    for hop in range(3, depth):
        f_event(hop)
    for b in range(batch):
        x_end(b)
    store_mixed(steps - 2).wait()
    store_mixed(steps - 1).wait()
    w_end()


def gather(queries, keys_in, values_in, out_weight, count):
    batch, tokens, heads, size = keys_in.shape
    depth, lanes = lax.axis_size("dp"), lax.axis_size("sp")
    places = lanes // 2
    rows, width = out_weight.shape
    held, deep = heads // 2, size + EXTRA
    tile = min(TILE, tokens)
    any_space = pl.BlockSpec(memory_space=pl.ANY)
    dma = pltpu.SemaphoreType.DMA
    f32, bf16 = jnp.float32, jnp.bfloat16
    w_dma = dma((2, depth, 2))
    return pl.pallas_call(
        functools.partial(
            gather_kernel, (depth, lanes), count, tile, batch, tokens, heads, size
        ),
        out_shape=(
            jax.ShapeDtypeStruct((batch * tokens, heads * size), bf16),
            jax.ShapeDtypeStruct((depth * rows, width), bf16),
        ),
        in_specs=[any_space] * 4,
        out_specs=(any_space, any_space),
        scratch_shapes=[
            pltpu.VMEM((SLOTS, tile, heads, size), bf16),
            pltpu.VMEM((SLOTS, tile, heads, size), bf16),
            pltpu.VMEM((SLOTS, tile, heads, size), bf16),
            pltpu.VMEM((2, tile, heads * size), bf16),
            pltpu.VMEM((tile * PITCH, size), f32),
            pltpu.VMEM((tile * PITCH, size), f32),
            pltpu.VMEM((batch, heads, deep, size), f32),
            pltpu.VMEM((batch, held, deep, size), f32),
            pltpu.VMEM((batch, held, deep, size), bf16),
            pltpu.VMEM((batch, places - 1, held // places, deep, size), bf16),
            pltpu.VMEM((batch, heads, deep, size), bf16),
            pltpu.VMEM((heads, 2 * size, 2 * size), bf16),
            pltpu.VMEM((depth, rows, width), bf16),
            dma((2, SLOTS)),
            dma((SLOTS,)),
            dma((2,)),
            dma,
            dma((2, depth)),
            w_dma, w_dma, w_dma, w_dma, w_dma, w_dma, w_dma, w_dma,
            dma((batch,)),
            dma((batch,)),
            dma((batch, places)),
            dma((batch, places)),
            dma((batch, places)),
            dma((batch, places)),
            dma((batch,)),
            dma((batch,)),
        ],
        compiler_params=pltpu.CompilerParams(
            collective_id=0, has_side_effects=True, vmem_limit_bytes=60 * 2**20
        ),
    )(queries, keys_in, values_in, out_weight)


def on_device(queries_in, keys_in, values_in, out_weight):
    batch, tokens = queries_in.shape[:2]
    count = tokens * lax.axis_size("sp")
    mixed, wide = gather(queries_in, keys_in, values_in, out_weight, count)
    out = jnp.dot(mixed, wide, preferred_element_type=jnp.float32).astype(jnp.bfloat16)
    return out.reshape(batch, tokens, wide.shape[1])


def solution(mesh):
    placed = (
        P("dp", "sp", None, None),
        P("dp", "sp", None, None),
        P("dp", "sp", None, None),
        P("dp", None),
    )
    return jax.shard_map(
        on_device, mesh=mesh, in_specs=placed, out_specs=P("dp", "sp", None), check_vma=False
    )
```

time: 88.1 us -> 81.5 us (0.925)
  Pallas kernels: 87.8 us -> 57.8 us
  matrix products: 0 us -> 23.5 us
    pallas_call x2 -> x1, Pallas kernels: 87.8 us -> 57.8 us  [gather(): pl.pallas_call(functools.partial(gather_kernel, (depth, lanes), count, ti...]
    dot_general x0 -> x1, matrix products: none -> 23.5 us  [on_device(): jnp.dot(mixed, wide, preferred_element_type=jnp.float32)]
where the time goes in v1:
time: 81.5 us; the launch traced here: 81.3 us
  Pallas kernels  57.8 us (71%)
  matrix products  23.5 us (29%)
    pallas_call x1, Pallas kernels, gather(): pl.pallas_call(functools.partial(gather_kernel, (depth, lanes), count, ti...  57.8 us
    dot_general x1, matrix products, on_device(): jnp.dot(mixed, wide, preferred_element_type=jnp.float32)  23.5 us

profile of v1, /device:TPU:9, one launch (start us, length us, event | category | flops | bytes accessed | tf_op | source)
XLA Modules:
  0.0 81.3 jit_solution(8055547402619363927)
XLA Ops:
  0.0 57.8 %shard_map.46 = (bf16[2048,2048]{1,0:T(8,128)(2,1)}, bf16[2048,2048]{1,0:T(8,128)(2,1)}) custom-call(bf16[2,1024,16,128]{3,2,1,0:T(8,128)(2,1)} %q_ref.1, bf16[2,1024,16,128]{3,2,1,0:T(8,128)(2,1)} %k_ref.1, bf16[2,1024,16,128]{3,2,1,0:T(8,128)(2,1)} %v_ref.1, bf16[512,2048]{1,0:T(8,128)(2,1)} %w_ref.1), custom_call_target="tpu_custom_call" | custom-call | tf_op jit(solution)/shard_map/pallas_call | solution.py:407
  57.8 23.5 %convolution_convert_fusion = bf16[2048,2048]{1,0:T(8,128)(2,1)} fusion(bf16[2048,2048]{1,0:T(8,128)(2,1)} %get-tuple-element.7, bf16[2048,2048]{1,0:T(8,128)(2,1)} %get-tuple-element.8), kind=kOutput, calls=%fused_computation | convolution fusion | flops 17184063488 | bytes 25165824 | tf_op jit(solution)/shard_map/dot_general | solution.py:456

commit v2 on v1

v2 whole, which is shorter than its diff:
```python
import functools

import jax
import jax.numpy as jnp
from jax import lax
from jax.experimental import pallas as pl
from jax.experimental.pallas import tpu as pltpu
from jax.sharding import PartitionSpec as P

MESH = pl.DeviceIdType.MESH
SLOTS = 3
TILE = 256
SUBLANES = 8
PITCH = 24
EXTRA = 16
CUTS = 2
GROUP = 32
REGIONS = 8
T_FOLD, T_Z = 4.0, 4.2
D_FOLD, D_PREPARE, D_TABLE, D_READ, D_PROJECT = 1.2, 0.75, 1.0, 0.8, 1.3
D_Z, D_N, D_C, D_R, D_G = 2.81, 4.5, 2.0, 5.6, 5.6


def feature_map(values):
    wide = values.astype(jnp.float32)
    return wide * wide + 0.1


def split_mass(mass):
    high = mass.astype(jnp.bfloat16).astype(jnp.float32)
    row = lax.broadcasted_iota(jnp.int32, mass.shape, mass.ndim - 2)
    return jnp.where(row % 2 == 0, high, mass - high).astype(jnp.bfloat16)


def gather_kernel(
    groups, count, tile, batch, tokens, heads, size,
    q_ref, k_ref, v_ref, w_ref, mixed, w_all, acc,
    k_buf, v_buf, q_buf, regions, rel_k, total, core_in, out_buf, in_buf,
    final, table, load_sem, q_sem, own_sem,
    z_send, z_recv, n_send, n_recv, p_send, p_recv, m_send, m_recv,
    c_send, c_recv, r_send, r_recv, g_send, g_recv, f_send, f_recv,
):
    f32, bf16 = jnp.float32, jnp.bfloat16
    depth, lanes = groups
    places = lanes // 2
    levels = places.bit_length() - 1
    d, s = lax.axis_index("dp"), lax.axis_index("sp")
    core, place = s % 2, s // 2
    rows, width = w_ref.shape
    part, half_width = rows // 4, width // 2
    cut = part // CUTS
    pieces = [(r, side) for r in range(CUTS) for side in range(2)]
    per_batch = tokens // tile
    steps = batch * per_batch
    held = heads // 2
    piece = held // places
    root = count**0.5

    def flip(value, bit):
        return value + (1 << bit) - 2 * (1 << bit) * ((value // (1 << bit)) % 2)

    def peer_place(k):
        other = place
        for bit in range(levels):
            if k >> bit & 1:
                other = flip(other, bit)
        return other

    partner = {"sp": flip(s, 0)}
    peers = [{"sp": 2 * peer_place(k) + core} for k in range(1, places)]
    sides = [{"sp": flip(s, 1)}, {"sp": flip(s, levels)}]
    parity = place % 2
    if levels > 1:
        parity = (parity + (place // (1 << (levels - 1))) % 2) % 2
    quarter, across = parity * 2 + core, (1 - parity) * 2 + core

    barrier = pltpu.get_barrier_semaphore()
    for device in [partner] + peers + [{"dp": (d + k) % depth} for k in (1, depth - 1)]:
        pl.semaphore_signal(barrier, inc=1, device_id=device, device_id_type=MESH)

    def load(i):
        b, t, slot = i // per_batch, i % per_batch, i % SLOTS
        at = pl.ds(t * tile, tile)
        return (
            pltpu.make_async_copy(k_ref.at[b, at], k_buf.at[slot], load_sem.at[0, slot]),
            pltpu.make_async_copy(v_ref.at[b, at], v_buf.at[slot], load_sem.at[1, slot]),
        )

    def load_q(i):
        b, t, slot = i // per_batch, i % per_batch, i % SLOTS
        return pltpu.make_async_copy(
            q_ref.at[b, pl.ds(t * tile, tile)], q_buf.at[slot], q_sem.at[slot]
        )

    for i in range(min(SLOTS - 1, steps)):
        for copy in load(i):
            copy.start()
    own = pltpu.make_async_copy(w_ref, w_all.at[d], own_sem)
    own.start()
    total[...] = jnp.zeros_like(total)
    table[...] = jnp.zeros_like(table)
    pl.semaphore_wait(barrier, places + 2)

    def origin(way, hop):
        return d - hop if way == 0 else d + hop

    def inside(place_on_dp):
        return jnp.logical_and(place_on_dp >= 0, place_on_dp < depth)

    def sends(way, hop):
        return jnp.logical_and(inside(origin(way, hop - 1)), inside(origin(way, -1)))

    def block(from_dp, index, c):
        r, side = pieces[c]
        return w_all.at[
            from_dp, pl.ds(index * part + r * cut, cut), pl.ds(side * half_width, half_width)
        ]

    def z_copy(way, hop, c):
        target = block(origin(way, hop - 1), quarter, c)
        source = target
        if hop == 1:
            r, side = pieces[c]
            source = w_ref.at[
                pl.ds(quarter * part + r * cut, cut), pl.ds(side * half_width, half_width)
            ]
        return pltpu.make_async_remote_copy(
            src_ref=source, dst_ref=target,
            send_sem=z_send.at[way, hop, c], recv_sem=z_recv.at[way, hop, c],
            device_id={"dp": (d + (1 if way == 0 else depth - 1)) % depth},
            device_id_type=MESH,
        )

    def z_arrival(way, hop, c):
        target = block(origin(way, hop), quarter, c)
        return pltpu.make_async_remote_copy(
            src_ref=target, dst_ref=target,
            send_sem=z_send.at[way, hop, c], recv_sem=z_recv.at[way, hop, c],
            device_id={"dp": (d + 1) % depth}, device_id_type=MESH,
        )

    def spread(way, hop, c, index, send, recv, device):
        target = block(origin(way, hop), index, c)
        return pltpu.make_async_remote_copy(
            src_ref=target, dst_ref=target,
            send_sem=send.at[way, hop, c], recv_sem=recv.at[way, hop, c],
            device_id=device, device_id_type=MESH,
        )

    def n_copy(way, hop, c):
        return spread(way, hop, c, quarter, n_send, n_recv, sides[pieces[c][1]])

    def p_copy(way, hop, c):
        return spread(way, hop, c, quarter, p_send, p_recv, partner)

    def m_copy(way, hop, c):
        return spread(way, hop, c, across, m_send, m_recv, partner)

    def each_way(hop, act):
        for way in range(2):
            pl.when(inside(origin(way, hop)))(functools.partial(act, way))

    done = set()

    def once(*key):
        fresh = key[1] < depth and key not in done
        done.add(key)
        return fresh

    def z_event(hop, c):
        if not once("z", hop, c):
            return
        each_way(hop, lambda way: z_arrival(way, hop, c).wait_recv())
        if hop + 1 < depth:
            for way in range(2):
                pl.when(sends(way, hop + 1))(lambda way=way: z_copy(way, hop + 1, c).start())

        def forward(way):
            n_copy(way, hop, c).start()
            p_copy(way, hop, c).start()

        each_way(hop, forward)

    def n_event(hop, c):
        if not once("n", hop, c):
            return

        def act(way):
            n_copy(way, hop, c).wait_recv()
            m_copy(way, hop, c).start()

        each_way(hop, act)

    def f_event(hop):
        if not once("f", hop):
            return
        for c in range(len(pieces)):
            z_event(hop, c)
        for c in range(len(pieces)):
            n_event(hop, c)

        def act(way):
            for c in range(len(pieces)):
                p_copy(way, hop, c).wait_recv()
                m_copy(way, hop, c).wait_recv()

        each_way(hop, act)

    def w_end():
        for hop in range(1, depth):
            f_event(hop)
        for hop in range(1, depth):
            for way in range(2):
                for c in range(len(pieces)):
                    pl.when(sends(way, hop))(
                        lambda way=way, hop=hop, c=c: z_copy(way, hop, c).wait_send()
                    )

            def act(way, hop=hop):
                for c in range(len(pieces)):
                    for make in (n_copy, p_copy, m_copy):
                        make(way, hop, c).wait_send()

            each_way(hop, act)

    for c in range(len(pieces)):
        for way in range(2):
            pl.when(sends(way, 1))(lambda way=way, c=c: z_copy(way, 1, c).start())

    def c_copy(b):
        return pltpu.make_async_remote_copy(
            src_ref=total.at[b, pl.ds((1 - core) * held, held)], dst_ref=core_in.at[b],
            send_sem=c_send.at[b], recv_sem=c_recv.at[b],
            device_id=partner, device_id_type=MESH,
        )

    def r_copy(b, k):
        return pltpu.make_async_remote_copy(
            src_ref=out_buf.at[b, pl.ds(peer_place(k) * piece, piece)],
            dst_ref=in_buf.at[b, k - 1],
            send_sem=r_send.at[b, k], recv_sem=r_recv.at[b, k],
            device_id=peers[k - 1], device_id_type=MESH,
        )

    def g_copy(b, k):
        at = final.at[b, pl.ds(core * held + place * piece, piece)]
        return pltpu.make_async_remote_copy(
            src_ref=at, dst_ref=at, send_sem=g_send.at[b, k], recv_sem=g_recv.at[b, k],
            device_id=peers[k - 1], device_id_type=MESH,
        )

    def f_copy(b):
        at = final.at[b, pl.ds(core * held, held)]
        return pltpu.make_async_remote_copy(
            src_ref=at, dst_ref=at, send_sem=f_send.at[b], recv_sem=f_recv.at[b],
            device_id=partner, device_id_type=MESH,
        )

    def x_add(b):
        c_copy(b).wait()
        mine = pl.ds(core * held, held)
        summed = total[b, mine] + core_in[b]
        total[b, mine] = summed
        out_buf[b, :, :size] = summed[:, :size].astype(bf16)
        out_buf[b, :, size:] = split_mass(summed[:, size:])
        for k in range(1, places):
            r_copy(b, k).start()

    def x_sum(b):
        mine = pl.ds(core * held + place * piece, piece)
        state, mass = total[b, mine, :size], total[b, mine, size:]
        for k in range(1, places):
            r_copy(b, k).wait_recv()
            state += in_buf[b, k - 1, :, :size].astype(f32)
            pair = in_buf[b, k - 1, :, size:].astype(f32)
            mass += pair[:, :1] + pair[:, 1:2]
        final[b, mine, :size] = (state / count).astype(bf16)
        final[b, mine, size:] = split_mass(mass / count / root)
        for k in range(1, places):
            g_copy(b, k).start()

    def x_share(b):
        for k in range(1, places):
            g_copy(b, k).wait_recv()
        f_copy(b).start()

    def x_table(b):
        f_copy(b).wait_recv()
        for h in range(heads):
            pair = final[b, h, size:].astype(f32)
            table[h, :size, :size] = final[b, h, :size]
            table[h, size:, :size] = jnp.broadcast_to(pair[:1], (size, size)).astype(bf16)
            table[h, size:, size:] = jnp.broadcast_to(pair[1:2], (size, size)).astype(bf16)

    def x_end(b):
        for k in range(1, places):
            r_copy(b, k).wait_send()
            g_copy(b, k).wait_send()
        f_copy(b).wait_send()

    groups_of = tile // GROUP

    def regroup(g, values, store):
        region = regions[g % REGIONS]
        for part_of in range(heads // SUBLANES):
            start = part_of * SUBLANES
            region.at[part_of].reshape(GROUP, SUBLANES, size)[...] = values[
                :, start : start + SUBLANES
            ]
        for h in range(heads):
            line = pl.ds(h % SUBLANES, GROUP, stride=SUBLANES)
            store(h, region[h // SUBLANES, line, :].astype(bf16))

    ones = jnp.ones((EXTRA, tile), bf16)

    def fold(i):
        slot, b = i % SLOTS, i // per_batch
        rel_k.reshape(tile, PITCH, size)[:, :heads, :] = feature_map(k_buf[slot])
        v_heads = pltpu.einshape("thd->htd", v_buf[slot])
        for h in range(heads):
            left = jnp.concatenate([jnp.transpose(v_heads[h]), ones], axis=0)
            right = rel_k[pl.ds(h, tile, stride=PITCH), :].astype(bf16)
            total[b, h] += jnp.dot(left, right, preferred_element_type=f32)

    def spot(i, h):
        block_of, column = divmod(h * size, rows)
        return block_of, pl.ds(i * tile, tile), pl.ds(column, size)

    def prepare(i):
        for g in range(groups_of):
            def put(h, x, g=g):
                block_of, column = divmod(h * size, rows)
                at = pl.ds(i * tile + g * GROUP, GROUP)
                mixed[block_of, at, pl.ds(column, size)] = x

            regroup(g, feature_map(q_buf[i % SLOTS, pl.ds(g * GROUP, GROUP)]), put)

    def read(i):
        for h in range(heads):
            feature = mixed[spot(i, h)]
            both = lax.dot_general(
                jnp.concatenate([feature, feature], axis=1), table[h],
                (((1,), (1,)), ((), ())), preferred_element_type=f32,
            )
            top = both[:, :size] / (both[:, size:] + 0.001 / root)
            mixed[spot(i, h)] = top.astype(bf16)

    broad = min(2 * tile, tokens)

    def project(i, j):
        at, source = pl.ds(i * broad, broad), nearest(d, depth, j)
        product = jnp.dot(mixed[source, at], w_all[source], preferred_element_type=f32)
        acc[at, :] = product if j == 0 else acc[at, :] + product

    def at_step(i, events):
        for moment, items in events.items():
            if not items:
                continue

            def run(items=items):
                for item in items:
                    item()

            pl.when(i == moment)(run)

    def make(function, *args):
        return functools.partial(function, *args)

    plan, clock = [], [T_FOLD]

    def due():
        now = []
        while plan and plan[0][0] <= clock[0]:
            now.append(plan.pop(0)[1])
        return now

    def run_due():
        for event in due():
            event()

    def loop(start, stop, body, length, extra=None):
        events = {}
        for i in range(start, stop):
            events[i] = (extra or {}).get(i, []) + due()
            clock[0] += length

        def one(i, carry):
            at_step(i, events)
            body(i)
            return carry

        lax.fori_loop(start, stop, one, 0)

    def fold_step(i):
        @pl.when(i + SLOTS - 1 < steps)
        def _():
            for copy in load(i + SLOTS - 1):
                copy.start()

        @pl.when(i + SLOTS - 1 >= steps)
        def _():
            load_q(i + SLOTS - 1 - steps).start()

        for copy in load(i):
            copy.wait()
        fold(i)

    def prepare_step(i):
        @pl.when(i + SLOTS - 1 < steps)
        def _():
            load_q(i + SLOTS - 1).start()

        load_q(i).wait()
        prepare(i)

    half = per_batch
    t_half = T_FOLD + half * D_FOLD
    t_full = T_FOLD + steps * D_FOLD
    for hop in range(1, depth):
        for c in range(len(pieces)):
            arrival = T_Z + D_Z * (len(pieces) * (hop - 1) + c + 1)
            plan.append((arrival, make(z_event, hop, c)))
            plan.append((arrival + D_N, make(n_event, hop, c)))
    plan.append((t_half + D_C, make(x_add, 0)))
    plan.append((t_half + D_C + D_R, make(x_sum, 0)))
    plan.append((t_half + D_C + D_R + D_G, make(x_share, 0)))
    plan.append((t_full + D_C, make(x_add, 1)))
    plan.append((t_full + D_C + D_R, make(x_sum, 1)))
    plan.append((t_full + D_C + D_R + D_G, make(x_share, 1)))
    plan.sort(key=lambda item: item[0])

    def require(name, b):
        for index, item in enumerate(plan):
            if item[1].func is name and item[1].args == (b,):
                for _ in range(index + 1):
                    plan.pop(0)[1]()
                clock[0] = max(clock[0], item[0])
                return

    loop(0, steps, fold_step, D_FOLD, {half: [lambda: c_copy(0).start()]})
    c_copy(1).start()
    loop(0, steps, prepare_step, D_PREPARE)
    own.wait()
    require(x_share, 0)
    run_due()
    x_table(0)
    clock[0] += D_TABLE
    loop(0, half, read, D_READ)
    mid = half * tile // broad
    end = 2 * mid
    loop(0, mid, lambda i: project(i, 0), D_PROJECT)
    require(x_share, 1)
    run_due()
    x_table(1)
    clock[0] += D_TABLE
    loop(half, steps, read, D_READ)
    loop(mid, end, lambda i: project(i, 0), D_PROJECT)
    for j in range(1, depth - 1):
        f_event(j)
        loop(0, end, lambda i, j=j: project(i, j), D_PROJECT)
    for b in range(batch):
        x_end(b)
    w_end()


def nearest(d, depth, j):
    both = 2 * jnp.minimum(d, depth - 1 - d)
    around = d - (j + 1) // 2 if j % 2 else d + j // 2
    return jnp.where(j <= both, around, jnp.where(d < depth - 1 - d, j, depth - 1 - j))


def close_kernel(depth, tile, acc, mixed, w_all, out_ref, stage, sem):
    source = nearest(lax.axis_index("dp"), depth, depth - 1)
    steps = acc.shape[0] // tile

    def store(i):
        return pltpu.make_async_copy(
            stage.at[i % 2], out_ref.at[pl.ds(i * tile, tile)], sem.at[i % 2]
        )

    def step(i, carry):
        at = pl.ds(i * tile, tile)
        pl.when(i > 1)(lambda: store(i - 2).wait())
        product = jnp.dot(mixed[source, at], w_all[source], preferred_element_type=jnp.float32)
        stage[i % 2] = (acc[at, :] + product).astype(jnp.bfloat16)
        store(i).start()
        return carry

    lax.fori_loop(0, steps, step, 0)
    for i in range(max(steps - 2, 0), steps):
        store(i).wait()


def close(acc, mixed, w_all, tile):
    vmem = pl.BlockSpec(memory_space=pltpu.VMEM)
    total, width = acc.shape
    return pl.pallas_call(
        functools.partial(close_kernel, w_all.shape[0], tile),
        out_shape=jax.ShapeDtypeStruct((total, width), jnp.bfloat16),
        in_specs=[vmem] * 3,
        out_specs=pl.BlockSpec(memory_space=pl.ANY),
        scratch_shapes=[
            pltpu.VMEM((2, tile, width), jnp.bfloat16),
            pltpu.SemaphoreType.DMA((2,)),
        ],
        compiler_params=pltpu.CompilerParams(vmem_limit_bytes=8 * 2**20),
    )(acc, mixed, w_all)


def gather(queries, keys_in, values_in, out_weight, count):
    batch, tokens, heads, size = keys_in.shape
    depth, lanes = lax.axis_size("dp"), lax.axis_size("sp")
    places = lanes // 2
    rows, width = out_weight.shape
    held, deep = heads // 2, size + EXTRA
    tile = min(TILE, tokens)
    any_space = pl.BlockSpec(memory_space=pl.ANY)
    dma = pltpu.SemaphoreType.DMA
    f32, bf16 = jnp.float32, jnp.bfloat16
    w_dma = dma((2, depth, 2 * CUTS))
    vmem = pl.BlockSpec(memory_space=pltpu.VMEM)
    return pl.pallas_call(
        functools.partial(
            gather_kernel, (depth, lanes), count, tile, batch, tokens, heads, size
        ),
        out_shape=(
            pltpu.VMEM((depth, batch * tokens, rows), bf16),
            pltpu.VMEM((depth, rows, width), bf16),
            pltpu.VMEM((batch * tokens, width), f32),
        ),
        in_specs=[any_space] * 4,
        out_specs=(vmem, vmem, vmem),
        scratch_shapes=[
            pltpu.VMEM((SLOTS, tile, heads, size), bf16),
            pltpu.VMEM((SLOTS, tile, heads, size), bf16),
            pltpu.VMEM((SLOTS, tile, heads, size), bf16),
            [pltpu.VMEM((heads // SUBLANES, GROUP * SUBLANES, size), f32)] * REGIONS,
            pltpu.VMEM((tile * PITCH, size), f32),
            pltpu.VMEM((batch, heads, deep, size), f32),
            pltpu.VMEM((batch, held, deep, size), f32),
            pltpu.VMEM((batch, held, deep, size), bf16),
            pltpu.VMEM((batch, places - 1, held // places, deep, size), bf16),
            pltpu.VMEM((batch, heads, deep, size), bf16),
            pltpu.VMEM((heads, 2 * size, 2 * size), bf16),
            dma((2, SLOTS)),
            dma((SLOTS,)),
            dma,
            w_dma, w_dma, w_dma, w_dma, w_dma, w_dma, w_dma, w_dma,
            dma((batch,)),
            dma((batch,)),
            dma((batch, places)),
            dma((batch, places)),
            dma((batch, places)),
            dma((batch, places)),
            dma((batch,)),
            dma((batch,)),
        ],
        compiler_params=pltpu.CompilerParams(
            collective_id=0, has_side_effects=True, vmem_limit_bytes=26 * 2**20
        ),
    )(queries, keys_in, values_in, out_weight)


def on_device(queries_in, keys_in, values_in, out_weight):
    batch, tokens = queries_in.shape[:2]
    count = tokens * lax.axis_size("sp")
    mixed, w_all, acc = gather(queries_in, keys_in, values_in, out_weight, count)
    out = close(acc, mixed, w_all, min(2 * TILE, tokens))
    return out.reshape(batch, tokens, out_weight.shape[1])


def solution(mesh):
    placed = (
        P("dp", "sp", None, None),
        P("dp", "sp", None, None),
        P("dp", "sp", None, None),
        P("dp", None),
    )
    return jax.shard_map(
        on_device, mesh=mesh, in_specs=placed, out_specs=P("dp", "sp", None), check_vma=False
    )
```

time: 81.5 us -> 68.8 us (0.84)
  matrix products: 23.5 us -> 0 us
  Pallas kernels: 57.8 us -> 68.7 us
    dot_general x1 -> x0, matrix products: 23.5 us -> none  [on_device(): jnp.dot(mixed, wide, preferred_element_type=jnp.float32)]
    pallas_call x0 -> x1, Pallas kernels: none -> 6.46 us  [close(): pl.pallas_call(functools.partial(close_kernel, w_all.shape[0], tile), out...]
    pallas_call x1, Pallas kernels: 57.8 us -> 62.2 us  [gather(): pl.pallas_call(functools.partial(gather_kernel, (depth, lanes), count, ti...]
where the time goes in v2:
time: 68.8 us; the launch traced here: 68.7 us
  Pallas kernels  68.7 us (100%)
    pallas_call x1, Pallas kernels, gather(): pl.pallas_call(functools.partial(gather_kernel, (depth, lanes), count, ti...  62.2 us
    pallas_call x1, Pallas kernels, close(): pl.pallas_call(functools.partial(close_kernel, w_all.shape[0], tile), out...  6.46 us

profile of v2, /device:TPU:9, one launch (start us, length us, event | category | flops | bytes accessed | tf_op | source)
XLA Modules:
  0.0 68.7 jit_solution(2816106599039608516)
XLA Ops:
  0.0 62.2 %shard_map.46 = (bf16[4,2048,512]{2,1,0:T(8,128)(2,1)S(1)}, bf16[4,512,2048]{2,1,0:T(8,128)(2,1)S(1)}, f32[2048,2048]{1,0:T(8,128)S(1)}) custom-call(bf16[2,1024,16,128]{3,2,1,0:T(8,128)(2,1)} %q_ref.1, bf16[2,1024,16,128]{3,2,1,0:T(8,128)(2,1)} %k_ref.1, bf16[2,1024,16,128]{3,2,1,0:T(8,128)(2,1)} %v_ref.1, bf16[512,2048]{1,0:T(8,128)(2,1)} %w_ref.1), custom_call_target="tpu_custom_call" | custom-call | tf_op jit(solution)/shard_map/pallas_call | solution.py:522
  62.2 6.5 %shard_map.47 = bf16[2048,2048]{1,0:T(8,128)(2,1)} custom-call(f32[2048,2048]{1,0:T(8,128)S(1)} %get-tuple-element.8.acc, bf16[4,2048,512]{2,1,0:T(8,128)(2,1)S(1)} %get-tuple-element.9.mixed, bf16[4,512,2048]{2,1,0:T(8,128)(2,1)S(1)} %get-tuple-element.10.w_all), custom_call_target="tpu_custom_call" | custom-call | tf_op jit(solution)/shard_map/pallas_call | solution.py:497

commit v3 on v2

--- a/solution.py
+++ b/solution.py
@@ -16,9 +16,10 @@
 CUTS = 2
 GROUP = 32
 REGIONS = 8
-T_FOLD, T_Z = 4.0, 4.2
+T_FOLD, T_Z = 4.0, 6.0
 D_FOLD, D_PREPARE, D_TABLE, D_READ, D_PROJECT = 1.2, 0.75, 1.0, 0.8, 1.3
-D_Z, D_N, D_C, D_R, D_G = 2.81, 4.5, 2.0, 5.6, 5.6
+D_Z, D_N, D_C, D_R, D_G = 2.81, 4.5, 1.8, 4.6, 4.6
+HOLD = 0.0
 
 
 def feature_map(values):
@@ -175,11 +176,15 @@
             for way in range(2):
                 pl.when(sends(way, hop + 1))(lambda way=way: z_copy(way, hop + 1, c).start())
 
-        def forward(way):
+    def s_event(hop, c):
+        if not once("s", hop, c):
+            return
+
+        def act(way):
             n_copy(way, hop, c).start()
             p_copy(way, hop, c).start()
 
-        each_way(hop, forward)
+        each_way(hop, act)
 
     def n_event(hop, c):
         if not once("n", hop, c):
@@ -194,10 +199,9 @@
     def f_event(hop):
         if not once("f", hop):
             return
-        for c in range(len(pieces)):
-            z_event(hop, c)
-        for c in range(len(pieces)):
-            n_event(hop, c)
+        for event in (z_event, s_event, n_event):
+            for c in range(len(pieces)):
+                event(hop, c)
 
         def act(way):
             for c in range(len(pieces)):
@@ -416,11 +420,15 @@
     half = per_batch
     t_half = T_FOLD + half * D_FOLD
     t_full = T_FOLD + steps * D_FOLD
+    free = [0.0, 0.0]
     for hop in range(1, depth):
         for c in range(len(pieces)):
             arrival = T_Z + D_Z * (len(pieces) * (hop - 1) + c + 1)
+            ready, side = max(arrival, HOLD), pieces[c][1]
+            free[side] = max(free[side], ready) + D_Z * (2 if hop == 1 else 1)
             plan.append((arrival, make(z_event, hop, c)))
-            plan.append((arrival + D_N, make(n_event, hop, c)))
+            plan.append((ready, make(s_event, hop, c)))
+            plan.append((free[side] + D_N, make(n_event, hop, c)))
     plan.append((t_half + D_C, make(x_add, 0)))
     plan.append((t_half + D_C + D_R, make(x_sum, 0)))
     plan.append((t_half + D_C + D_R + D_G, make(x_share, 0)))

time: 68.8 us -> 65.2 us (0.948)
  Pallas kernels: 68.7 us -> 64.8 us
    pallas_call x1, Pallas kernels: 62.2 us -> 58.3 us  [gather(): pl.pallas_call(functools.partial(gather_kernel, (depth, lanes), count, ti...]
where the time goes in v3:
time: 65.2 us; the launch traced here: 64.8 us
  Pallas kernels  64.8 us (99%)
    pallas_call x1, Pallas kernels, gather(): pl.pallas_call(functools.partial(gather_kernel, (depth, lanes), count, ti...  58.3 us
    pallas_call x1, Pallas kernels, close(): pl.pallas_call(functools.partial(close_kernel, w_all.shape[0], tile), out...  6.46 us

profile of v3, /device:TPU:9, one launch (start us, length us, event | category | flops | bytes accessed | tf_op | source)
XLA Modules:
  0.0 64.8 jit_solution(6536079473725022875)
XLA Ops:
  0.0 58.3 %shard_map.46 = (bf16[4,2048,512]{2,1,0:T(8,128)(2,1)S(1)}, bf16[4,512,2048]{2,1,0:T(8,128)(2,1)S(1)}, f32[2048,2048]{1,0:T(8,128)S(1)}) custom-call(bf16[2,1024,16,128]{3,2,1,0:T(8,128)(2,1)} %q_ref.1, bf16[2,1024,16,128]{3,2,1,0:T(8,128)(2,1)} %k_ref.1, bf16[2,1024,16,128]{3,2,1,0:T(8,128)(2,1)} %v_ref.1, bf16[512,2048]{1,0:T(8,128)(2,1)} %w_ref.1), custom_call_target="tpu_custom_call" | custom-call | tf_op jit(solution)/shard_map/pallas_call | solution.py:530
  58.4 6.5 %shard_map.47 = bf16[2048,2048]{1,0:T(8,128)(2,1)} custom-call(f32[2048,2048]{1,0:T(8,128)S(1)} %get-tuple-element.8.acc, bf16[4,2048,512]{2,1,0:T(8,128)(2,1)S(1)} %get-tuple-element.9.mixed, bf16[4,512,2048]{2,1,0:T(8,128)(2,1)S(1)} %get-tuple-element.10.w_all), custom_call_target="tpu_custom_call" | custom-call | tf_op jit(solution)/shard_map/pallas_call | solution.py:505

commit v4 on v3

--- a/solution.py
+++ b/solution.py
@@ -16,7 +16,7 @@
 CUTS = 2
 GROUP = 32
 REGIONS = 8
-T_FOLD, T_Z = 4.0, 6.0
+T_FOLD, T_Z = 4.0, 5.0
 D_FOLD, D_PREPARE, D_TABLE, D_READ, D_PROJECT = 1.2, 0.75, 1.0, 0.8, 1.3
 D_Z, D_N, D_C, D_R, D_G = 2.81, 4.5, 1.8, 4.6, 4.6
 HOLD = 0.0

time: 65.2 us -> 64.5 us (0.989)
  no operation moved by 1% of the time
where the time goes in v4:
time: 64.5 us; the launch traced here: 64.4 us
  Pallas kernels  64.4 us (100%)
    pallas_call x1, Pallas kernels, gather(): pl.pallas_call(functools.partial(gather_kernel, (depth, lanes), count, ti...  57.9 us
    pallas_call x1, Pallas kernels, close(): pl.pallas_call(functools.partial(close_kernel, w_all.shape[0], tile), out...  6.46 us

profile of v4, /device:TPU:9, one launch (start us, length us, event | category | flops | bytes accessed | tf_op | source)
XLA Modules:
  0.0 64.4 jit_solution(15968647230039901438)
XLA Ops:
  0.0 57.9 %shard_map.46 = (bf16[4,2048,512]{2,1,0:T(8,128)(2,1)S(1)}, bf16[4,512,2048]{2,1,0:T(8,128)(2,1)S(1)}, f32[2048,2048]{1,0:T(8,128)S(1)}) custom-call(bf16[2,1024,16,128]{3,2,1,0:T(8,128)(2,1)} %q_ref.1, bf16[2,1024,16,128]{3,2,1,0:T(8,128)(2,1)} %k_ref.1, bf16[2,1024,16,128]{3,2,1,0:T(8,128)(2,1)} %v_ref.1, bf16[512,2048]{1,0:T(8,128)(2,1)} %w_ref.1), custom_call_target="tpu_custom_call" | custom-call | tf_op jit(solution)/shard_map/pallas_call | solution.py:530
  57.9 6.5 %shard_map.47 = bf16[2048,2048]{1,0:T(8,128)(2,1)} custom-call(f32[2048,2048]{1,0:T(8,128)S(1)} %get-tuple-element.8.acc, bf16[4,2048,512]{2,1,0:T(8,128)(2,1)S(1)} %get-tuple-element.9.mixed, bf16[4,512,2048]{2,1,0:T(8,128)(2,1)S(1)} %get-tuple-element.10.w_all), custom_call_target="tpu_custom_call" | custom-call | tf_op jit(solution)/shard_map/pallas_call | solution.py:505
